TPU v7x, 512 devices: a whole 4x8x8 slice. The times are simulated.
512 devices in a mesh: batch: 32 (over x, y), slab: 16 (over z, core).
Axes of the slice: x: 4, y: 8, z: 8, core: 2. Of those that a mesh axis runs over, the one named last changes fastest.
Arguments:
- volumes: float32 [64, 128, 128, 128], P('batch', 'slab'), may hold values from -6 to 6
- tilt_low: int32 [64], P('batch'), may hold values from -70 to -40
- tilt_high: int32 [64], P('batch'), may hold values from 40 to 70
- shifts: int32 [64, 3], P('batch'), may hold values from 0 to 127
- support: float32 [128, 128, 128], P('slab'), may hold values from 0.2 to 1
Outputs:
- average: float32 [128, 128, 128], P('slab')
- misfits: float32 [3], replicated
Inputs may be any that keep to these rules, and one draw needn't show every extreme that they name: `shifts`: columns hold the shift along z, y and x.
All inputs are finite; a program needn't handle non-finite values.
Results may differ from a plain program's by a relative error of at most 0.0003.
Values sent between devices are 32-bit elements; how exact they have to be, the bound alone decides.
A program may use at most 64 MiB of HBM per device.

v0:
```python
import functools
import math

import jax
import jax.numpy as jnp
import numpy as np
from jax import lax
from jax.experimental import pallas as pl
from jax.experimental.pallas import tpu as pltpu
from jax.sharding import PartitionSpec as P

ITERS = 3
REG_WEIGHT = 0.5
FLOOR_VALUE = 1.0
SOFTNESS = 5.0
MESH = pl.DeviceIdType.MESH
LANES = 128
HALF = LANES // 2
XS = 4
GROUP = XS * 2
CHUNKS = 4
F32 = jnp.float32
BF16 = jnp.bfloat16


def signed(length):
    index = np.arange(length)
    return np.where(index < length // 2, index, index - length)


def tables(depth, width):
    half = depth // 2
    kz, z = np.arange(half), np.arange(depth)
    angle = 2 * np.pi * (kz[:, None] * z[None, :] % depth) / depth
    scale = 1 / math.sqrt(depth)
    down = np.zeros((depth + 8, depth))
    down[:half], down[half:depth] = np.cos(angle) * scale, -np.sin(angle) * scale
    down[depth] = np.where(z % 2 == 0, 1, -1) * scale
    twice = np.where(kz == 0, 1, 2)[None, :]
    up = np.concatenate([np.cos(angle.T) * twice, -np.sin(angle.T) * twice], 1) * scale
    kx = np.arange(width)
    turn = 2 * np.pi * (kx[:, None] * kx[None, :] % width) / width
    across = np.concatenate([np.cos(turn), np.sin(turn)], 1) / math.sqrt(width)
    fz, fx = signed(depth), signed(width)
    theta = np.degrees(np.arctan2(fz[:, None] * np.where(fx >= 0, 1, -1)[None, :], np.abs(fx)[None, :] * 1.0))
    mirror = theta[(-z) % depth][:, (-kx) % width]
    rows = np.minimum(np.arange(half + 8), half)
    theta, mirror = theta[rows], mirror[rows]
    mirror[0], mirror[half:] = theta[0], theta[half:]
    shift = 2 * np.pi * (rows[:, None] * np.arange(LANES)[None, :] % depth) / depth
    wedge = [np.exp(theta / SOFTNESS), np.exp(-theta / SOFTNESS), np.exp(mirror / SOFTNESS), np.exp(-mirror / SOFTNESS)]
    count = np.zeros((depth + 8, LANES))
    count[:depth], count[depth : depth + 2] = 2, 1
    count[0] = count[half] = 1
    single = np.concatenate(wedge + [np.cos(shift), np.sin(shift), count, np.cos(turn), np.sin(turn)], 0)
    return split(down), split(across), split(up), single.astype(np.float32)


def split(table):
    table = table.astype(np.float32)
    high = table.astype(BF16)
    low = (table - high.astype(np.float32)).astype(BF16)
    return np.concatenate([high, low], 0)


def halves(value):
    high = value.astype(BF16)
    return high, (value - high.astype(F32)).astype(BF16)


def mul(a, b):
    return jnp.dot(a, b, preferred_element_type=F32)


def by_table(value, table):
    rows = table.shape[0] // 2
    high, low = halves(value)
    top = table[:rows]
    return mul(high, top) + mul(low, top) + mul(high, table[rows:])


def table_by(table, value):
    rows = table.shape[0] // 2
    high, low = halves(value)
    top = table[:rows]
    return mul(top, high) + mul(top, low) + mul(table[rows:], high)


def arrange(slabs, v_ref, s_ref, shift_ref, u_ref, b_ref):
    ys = slabs * 8
    batch = lax.axis_index("batch")
    ring = lax.axis_size("batch") // XS
    mine = (batch // ring) * 2 + batch % 2
    energy = jnp.zeros((8, LANES), F32)
    for item in range(2):
        turn = shift_ref[item, 1]

        def block(t, energy, item=item, turn=turn):
            for k in range(8):
                y = lax.rem(t * 8 + k - turn + 2 * ys, ys)
                rows = v_ref[pl.ds(item * 8 * ys + y, 8, stride=ys), :]
                u_ref[t, k, item] = rows
                energy = energy + rows * rows
            return energy

        energy = lax.fori_loop(0, slabs, block, energy)

    def place(t, carry):
        b_ref[t, 0:8] = s_ref[pl.ds(t * 8 + mine, 8, stride=ys), :]
        b_ref[t, 8:16] = energy
        return carry

    lax.fori_loop(0, slabs, place, 0)


def refine(
    slabs, ring, u_ref, b_ref, t_ref, shift_ref, down, across, up, single, out_ref, mis_ref,
    block_in, tilt_out, tilt_in, tilts_out, tilts_in, rows_in, factors, part, parts_in, own_out, own_in,
    some_out, some_in, more_out, more_in, plane, pieces_in, planes_in,
    s_block, r_block, s_tilt, r_tilt, s_tilts, r_tilts, s_rows, r_rows, s_part, r_part, s_own, r_own,
    s_some, r_some, s_more, r_more, s_piece, r_piece, s_plane, r_plane,
):
    depth = slabs * 8
    half = depth // 2
    tall = half + 8
    copies = ring // 2
    subs = float(GROUP * copies * 2)
    cells = float(depth * depth * LANES)
    batch, slab = lax.axis_index("batch"), lax.axis_index("slab")
    x, y = batch // ring, batch % ring
    r, p = y // 2, y % 2
    g = x * 2 + p

    def at_slab(t):
        return (batch, t)

    def at_group(k):
        return ((k // 2) * ring + r * 2 + k % 2, slab)

    def at_copy(k):
        return (x * ring + k * 2 + p, slab)

    def each(count, me, act):
        def step(k, carry):
            off = count // 2 + (1 - k % 2) * (k // 2) - (k % 2) * ((k + 1) // 2)
            act(lax.rem(me + off, count))
            return carry

        if count > 1:
            lax.fori_loop(0, count - 1, step, 0)

    def exchange(count, me, device, source, target, send, recv):
        def copy(k, slot):
            return pltpu.make_async_remote_copy(
                src_ref=source(k), dst_ref=target(slot), send_sem=send.at[k], recv_sem=recv.at[slot],
                device_id=device(k), device_id_type=MESH,
            )

        return (
            lambda: each(count, me, lambda k: copy(k, me).start()),
            lambda: each(count, me, lambda k: copy(k, k).wait_recv()),
            lambda: each(count, me, lambda k: copy(k, me).wait_send()),
        )

    barrier = pltpu.get_barrier_semaphore()
    for count, me, device in ((slabs, slab, at_slab), (GROUP, g, at_group), (copies, r, at_copy)):
        each(count, me, lambda k, device=device: pl.semaphore_signal(
            barrier, inc=1, device_id=device(k), device_id_type=MESH))
    pl.semaphore_wait(barrier, slabs - 1 + GROUP - 1 + copies - 1)

    block = exchange(slabs, slab, at_slab, lambda k: b_ref.at[k], lambda k: block_in.at[k], s_block, r_block)
    tilt = exchange(GROUP, g, at_group, lambda k: tilt_out, lambda k: tilt_in.at[k], s_tilt, r_tilt)
    tilts = exchange(copies, r, at_copy, lambda k: tilts_out, lambda k: tilts_in.at[k], s_tilts, r_tilts)
    own = exchange(copies, r, at_copy, lambda k: own_out, lambda k: own_in.at[k], s_own, r_own)
    piece = exchange(
        slabs, slab, at_slab, lambda k: plane.at[pl.ds(pl.multiple_of(k * 8, 8), 8)], lambda k: pieces_in.at[k], s_piece, r_piece)
    whole = exchange(GROUP, g, at_group, lambda k: pieces_in, lambda k: planes_in.at[k], s_plane, r_plane)

    def chunk_rows(c):
        q = lax.rem(x + 1 + c, XS)
        return q, exchange(
            slabs, slab, at_slab, lambda k: u_ref.at[k, pl.ds(q * 2, 2)],
            lambda k: rows_in.at[pl.ds(q * 2, 2), :, k], s_rows.at[c], r_rows.at[c])

    def part_copy(k):
        return pltpu.make_async_remote_copy(
            src_ref=part.at[k], dst_ref=parts_in.at[g], send_sem=s_part.at[k], recv_sem=r_part.at[g],
            device_id=at_group(k), device_id_type=MESH)

    def part_wait(k):
        return pltpu.make_async_remote_copy(
            src_ref=part.at[k], dst_ref=parts_in.at[k], send_sem=s_part.at[k], recv_sem=r_part.at[k],
            device_id=at_group(k), device_id_type=MESH)

    block[0]()
    for c in range(2):
        chunk_rows(c)[1][0]()

    block_in[slab] = b_ref[slab]
    for k in range(8):
        for item in range(2):
            rows_in[k, item, slab] = u_ref[slab, k, item]

    lane = lax.broadcasted_iota(jnp.int32, (half, LANES), 1)
    row = lax.broadcasted_iota(jnp.int32, (half, LANES), 0)
    here = lane % HALF == row
    left = lane < HALF
    tile_row = lax.broadcasted_iota(jnp.int32, (8, LANES), 0)
    wide = lax.broadcasted_iota(jnp.int32, (tall, LANES), 1)

    def table(k):
        return single[k * tall : (k + 1) * tall]

    def weight(p_table, q_table, low, high):
        return 1.0 / ((1.0 + p_table * high) * (1.0 + q_table * low))

    for item in range(2):
        low, high = t_ref[0:1, item : item + 1], t_ref[0:1, item + 2 : item + 3]
        w = weight(table(0), table(1), low, high)
        dw = weight(table(2), table(3), low, high) - w
        pick = wide == shift_ref[item, 0]
        zc = jnp.sum(jnp.where(pick, table(4), 0.0), axis=1, keepdims=True)
        zs = jnp.sum(jnp.where(pick, table(5), 0.0), axis=1, keepdims=True)
        first = 6 * tall + depth + 8
        xc = single[pl.ds(first + shift_ref[item, 2], 1), :]
        xs = single[pl.ds(first + LANES + shift_ref[item, 2], 1), :]
        cosine, sine = zc * xc - zs * xs, zs * xc + zc * xs
        factors[item, 0], factors[item, 1] = w * cosine, w * sine
        factors[item, 2], factors[item, 3] = dw * cosine, dw * sine

    block[1]()
    energy = block_in[0, 8:16]
    for k in range(1, slabs):
        energy = energy + block_in[k, 8:16]
    tilt_out[0:8] = t_ref[...]
    tilt_out[8:16] = energy
    tilt[0]()
    tilt_in[g] = tilt_out[...]

    def chunk(c):
        q, rows = chunk_rows(c)
        rows[1]()
        stack = []
        for k in range(2):
            for item in range(2):
                stack.append(table_by(down, rows_in[q * 2 + k, item].reshape(depth, LANES)))
        product = by_table(jnp.concatenate(stack, 0), across)
        for k in range(2):
            re = im = re_last = im_last = d_re = d_im = 0.0
            for item in range(2):
                at = (k * 2 + item) * (depth + 8)
                c_top, c_low, c_last = (product[at + a : at + b, :LANES] for a, b in ((0, half), (half, depth), (depth, depth + 8)))
                s_top, s_low, s_last = (product[at + a : at + b, LANES:] for a, b in ((0, half), (half, depth), (depth, depth + 8)))
                a, b = c_top + s_low, c_low - s_top
                wc, ws = factors[item, 0, :half], factors[item, 1, :half]
                re, im = re + wc * a + ws * b, im + wc * b - ws * a
                wc, ws = factors[item, 2, :half], factors[item, 3, :half]
                d_re, d_im = d_re + wc * a + ws * b, d_im + wc * b - ws * a
                wc, ws = factors[item, 0, half:], factors[item, 1, half:]
                re_last, im_last = re_last + wc * c_last - ws * s_last, im_last - wc * s_last - ws * c_last

            def lying(d):
                column = jnp.where(left, d[:, 0:1], d[:, HALF : HALF + 1])
                return jnp.sum(jnp.where(here, column, 0.0), axis=0, keepdims=True)

            last = jnp.where(tile_row == 0, re_last[0:1], jnp.where(tile_row == 1, im_last[0:1], 0.0))
            last = jnp.where(tile_row == 2, lying(d_re), jnp.where(tile_row == 3, lying(d_im), last))
            part[q * 2 + k, 0:half], part[q * 2 + k, half:depth] = re, im
            part[q * 2 + k, depth:] = last
        return q

    def add_up(ref, count):
        total = ref[0]
        for k in range(1, count):
            total = total + ref[k]
        return total

    for c in range(CHUNKS):
        q = chunk(c)
        if c < CHUNKS - 1:
            part_copy(q * 2 + (1 - p)).start()
            part_copy(q * 2 + p).start()
        else:
            part_copy(q * 2 + (1 - p)).start()
        if c + 2 < CHUNKS:
            chunk_rows(c + 2)[1][0]()
        if c == 0:
            tilt[1]()
            tilts_out[0:8] = jnp.concatenate([tilt_in[k, 0:1] for k in range(GROUP)], 0)
            energy = tilt_in[0, 8:16]
            for k in range(1, GROUP):
                energy = energy + tilt_in[k, 8:16]
            tilts_out[8:16] = energy
            tilts[0]()
            tilts_in[r] = tilts_out[...]
        if c == 2:
            tilts[1]()
            energy = tilts_in[0, 8:16]
            for k in range(1, copies):
                energy = energy + tilts_in[k, 8:16]

            def square(k, totals):
                total, mirrored = totals
                for j in range(GROUP):
                    for item in range(2):
                        low, high = tilts_in[k, j : j + 1, item : item + 1], tilts_in[k, j : j + 1, item + 2 : item + 3]
                        w = weight(table(0), table(1), low, high)
                        total = total + w * w
                        w = weight(table(2), table(3), low, high)
                        mirrored = mirrored + w * w
                return total, mirrored

            none = jnp.zeros((tall, LANES), F32)
            total, mirrored = lax.fori_loop(0, copies, square, (none, none))

    parts_in[g] = part[g]
    each(GROUP, g, lambda k: part_wait(k).wait_recv())
    own_out[...] = add_up(parts_in, GROUP)
    own[0]()
    own_in[r] = own_out[...]

    def stacked(d):
        return jnp.concatenate([d[:half], d[:half], jnp.where(tile_row < 2, d[half : half + 1], 0.0)], 0)

    d_one, d_two = stacked(total), stacked(mirrored)
    support = block_in[:, 0:8].reshape(depth, LANES)
    sign = jnp.where(lax.broadcasted_iota(jnp.int32, (depth, LANES), 0) % 2 == 0, 1.0, -1.0) * (1 / math.sqrt(depth))
    count = single[6 * tall : 6 * tall + depth + 8]
    own[1]()
    sums = add_up(own_in, copies)

    def standing(values):
        spread = jnp.where(here, values, 0.0)
        one = jnp.sum(jnp.where(left, spread, 0.0), axis=1, keepdims=True)
        two = jnp.sum(jnp.where(left, 0.0, spread), axis=1, keepdims=True)
        return jnp.where(lane == 0, one, jnp.where(lane == HALF, two, 0.0))

    change = jnp.concatenate(
        [standing(sums[depth + 2 : depth + 3]), standing(sums[depth + 3 : depth + 4]), jnp.zeros((8, LANES), F32)], 0)
    sums = jnp.concatenate([sums[:depth], jnp.where(tile_row < 2, sums[depth:], 0.0)], 0)
    mean = jnp.zeros((depth + 8, LANES), F32)
    power = jnp.sum(energy, axis=(0, 1), keepdims=True)
    misfit = power * (1.0 / (subs * cells))
    misfits = jnp.where(tile_row == 0, misfit, 0.0)
    for turn in range(ITERS):
        damping = REG_WEIGHT * subs * misfit + FLOOR_VALUE
        one, two = 0.5 / (d_one + damping), 0.5 / (d_two + damping)
        update = mean - mean * (d_one * one + d_two * two) + (one + two) * sums + two * change
        product = by_table(update, across)
        re = product[:half, :LANES] - product[half:depth, LANES:]
        im = product[half:depth, :LANES] + product[:half, LANES:]
        last = product[depth : depth + 1, :LANES] - product[depth + 1 : depth + 2, LANES:]
        average = support * (table_by(up, jnp.concatenate([re, im], 0)) + sign * last)
        if turn + 1 == ITERS:
            break
        product = by_table(table_by(down, average), across)
        last = jnp.where(tile_row == 0, product[depth : depth + 1, :LANES], -product[depth : depth + 1, LANES:])
        mean = jnp.concatenate([
            product[:half, :LANES] + product[half:depth, LANES:],
            product[half:depth, :LANES] - product[:half, LANES:],
            jnp.where(tile_row < 2, last, 0.0)], 0)
        terms = count * mean * (0.5 * (d_one + d_two) * mean - 2.0 * sums - change)
        some_out[turn] = jnp.sum(terms.reshape(depth // 8 + 1, 8, LANES), axis=0)
        some = exchange(
            GROUP, g, at_group, lambda k: some_out.at[turn], lambda k: some_in.at[turn, k], s_some.at[turn], r_some.at[turn])
        some[0]()
        some_in[turn, g] = some_out[turn]
        some[1]()
        more_out[turn] = add_up(some_in.at[turn], GROUP)
        more = exchange(
            slabs, slab, at_slab, lambda k: more_out.at[turn], lambda k: more_in.at[turn, k], s_more.at[turn], r_more.at[turn])
        more[0]()
        more_in[turn, slab] = more_out[turn]
        more[1]()
        misfit = (power + jnp.sum(add_up(more_in.at[turn], slabs), axis=(0, 1), keepdims=True)) * (1.0 / (subs * cells))
        misfits = jnp.where(tile_row == turn + 1, misfit, misfits)
        some[2]()
        more[2]()
    mis_ref[...] = misfits
    plane[...] = average
    piece[0]()
    pieces_in[slab] = plane[pl.ds(pl.multiple_of(slab * 8, 8), 8)]
    piece[1]()
    whole[0]()

    def place(k, source):
        for j in range(slabs):
            out_ref[pl.ds(j * 8 + k, 8, stride=depth), :] = source[j]

    place(g, pieces_in)
    block[2](), tilt[2](), tilts[2](), own[2](), piece[2]()
    for c in range(CHUNKS):
        chunk_rows(c)[1][2]()
    each(GROUP, g, lambda k: part_wait(k).wait_send())
    whole[1]()
    each(GROUP, g, lambda k: place(k, planes_in.at[k]))
    whole[2]()


def body(volumes, tilt_low, tilt_high, shifts, support):
    slabs, ring = lax.axis_size("slab"), lax.axis_size("batch") // XS
    layer, ys, width = support.shape
    depth, copies, tall = layer * slabs, ring // 2, slabs * 8 + 8
    vmem, smem = pl.BlockSpec(memory_space=pltpu.VMEM), pl.BlockSpec(memory_space=pltpu.SMEM)
    u, blocks = pl.pallas_call(
        functools.partial(arrange, slabs),
        out_shape=(
            jax.ShapeDtypeStruct((slabs, 8, 2, 8, LANES), F32),
            jax.ShapeDtypeStruct((slabs, 16, LANES), F32),
        ),
        in_specs=[vmem, vmem, smem],
        out_specs=(vmem, vmem),
        name="arrange",
    )(volumes.reshape(2 * layer * ys, width), support.reshape(layer * ys, width), shifts)
    edges = jnp.concatenate(
        [jnp.exp(tilt_low.astype(F32) / SOFTNESS), jnp.exp(-tilt_high.astype(F32) / SOFTNESS)])
    edges = jnp.pad(edges[None, :], ((0, 7), (0, LANES - 4)))
    dma = pltpu.SemaphoreType.DMA

    def buffer(*shape):
        return pltpu.VMEM((*shape, LANES), F32)

    average, misfits = pl.pallas_call(
        functools.partial(refine, slabs, ring),
        out_shape=(
            jax.ShapeDtypeStruct((layer * ys, width), F32),
            jax.ShapeDtypeStruct((8, LANES), F32),
        ),
        in_specs=[vmem, vmem, vmem, smem, vmem, vmem, vmem, vmem],
        out_specs=(vmem, vmem),
        scratch_shapes=[
            buffer(slabs, 16), buffer(16), buffer(GROUP, 16), buffer(16), buffer(copies, 16),
            buffer(8, 2, slabs, 8), buffer(2, 4, depth // 2 + 8),
            buffer(GROUP, tall), buffer(GROUP, tall), buffer(tall), buffer(copies, tall),
            buffer(2, 8), buffer(2, GROUP, 8), buffer(2, 8), buffer(2, slabs, 8),
            buffer(depth), buffer(slabs, 8), buffer(GROUP, slabs, 8),
            dma((slabs,)), dma((slabs,)), dma((GROUP,)), dma((GROUP,)), dma((copies,)), dma((copies,)),
            dma((CHUNKS, slabs)), dma((CHUNKS, slabs)), dma((GROUP,)), dma((GROUP,)), dma((copies,)), dma((copies,)),
            dma((2, GROUP)), dma((2, GROUP)), dma((2, slabs)), dma((2, slabs)),
            dma((slabs,)), dma((slabs,)), dma((GROUP,)), dma((GROUP,)),
        ],
        compiler_params=pltpu.CompilerParams(collective_id=0, has_side_effects=True),
        name="refine",
    )(u, blocks, edges, shifts, *(jnp.asarray(t) for t in tables(depth, width)))
    return average.reshape(layer, ys, width), misfits[:ITERS, 0]


def solution(mesh):
    placed = (
        P("batch", "slab", None, None),
        P("batch"),
        P("batch"),
        P("batch", None),
        P("slab", None, None),
    )
    return jax.shard_map(
        body, mesh=mesh, in_specs=placed, out_specs=(P("slab", None, None), P()), check_vma=False
    )
```

profile of v0, /device:TPU:1, one launch (start us, length us, event | category | flops | bytes accessed | tf_op | source)
XLA Modules:
  0.0 103.6 jit_solution(650297828308430)
XLA Ops:
  0.6 0.0 copy-start.1
  0.6 0.0 copy-start.2
  0.6 0.6 copy-done.1
  1.3 0.0 copy-done.2
  1.3 0.1 maximum_bitcast_fusion
  1.4 0.6 pad.4.t_ref
  2.0 3.9 %arrange.1 = (f32[16,8,2,8,128]{4,3,2,1,0:T(8,128)}, f32[16,16,128]{2,1,0:T(8,128)}) custom-call(f32[2048,128]{1,0:T(8,128)} %bitcast.5, f32[1024,128]{1,0:T(8,128)} %bitcast.7, s32[2,3]{1,0:T(2,128)} %shift_ref.3), custom_call_target="tpu_custom_call" | custom-call | tf_op jit(solution)/shard_map/arrange/pallas_call | solution.py:405
  5.9 94.5 %refine.1 = (f32[1024,128]{1,0:T(8,128)}, f32[8,128]{1,0:T(8,128)}) custom-call(f32[16,8,2,8,128]{4,3,2,1,0:T(8,128)} %get-tuple-element.6.u_ref, f32[16,16,128]{2,1,0:T(8,128)} %get-tuple-element.7.b_ref, f32[8,128]{1,0:T(8,128)} %pad.4.t_ref, s32[2,3]{1,0:T(2,128)} %shift_ref.3, bf16[272,128]{1,0:T(8,128)(2,1)} %constant.15.clone.down, ...), custom_call_target="tpu_custom_call" | custom-call | tf_op jit(solution)/shard_map/refine/pallas_call | solution.py:423
  100.4 0.0 copy-start
  100.5 0.7 copy-done
  101.1 0.6 slice_reduce_fusion
  101.8 1.9 %copy.12 = f32[8,128,128]{2,1,0:T(8,128)} copy(f32[8,128,128]{2,1,0:T(8,128)} %bitcast.6) | data formatting | bytes 1048576
  (1 shorter events, 0.0 us)
Async XLA Ops:
  0.6 0.7 copy-start.1
  0.6 0.7 copy-start.2
  100.4 0.7 copy-start
where the time goes:
time: 104 us
  Pallas kernels  98.5 us (95%)
  local copies, waits for them, and re-layouts  4.42 us (4%)
    pallas_call x1, Pallas kernels, body(): pl.pallas_call(functools.partial(refine, slabs, ring), out_shape=(jax.Sha...  94.5 us
    pallas_call x1, Pallas kernels, body(): pl.pallas_call(functools.partial(arrange, slabs), out_shape=(jax.ShapeDty...  3.95 us
    unnamed x7, local copies, waits for them, and re-layouts  3.2 us

commit v1 on v0

v1 whole, which is shorter than its diff:
```python
import functools
import math

import jax
import jax.numpy as jnp
import numpy as np
from jax import lax
from jax.experimental import pallas as pl
from jax.experimental.pallas import tpu as pltpu
from jax.sharding import PartitionSpec as P

ITERS = 3
REG_WEIGHT = 0.5
FLOOR_VALUE = 1.0
SOFTNESS = 5.0
MESH = pl.DeviceIdType.MESH
LANES = 128
HALF = LANES // 2
XS = 4
GROUP = XS * 2
CHUNKS = 5
F32 = jnp.float32
BF16 = jnp.bfloat16


def signed(length):
    index = np.arange(length)
    return np.where(index < length // 2, index, index - length)


def tables(depth, width):
    half = depth // 2
    kz, z = np.arange(half), np.arange(depth)
    angle = 2 * np.pi * (kz[:, None] * z[None, :] % depth) / depth
    scale = 1 / math.sqrt(depth)
    down = np.zeros((depth + 8, depth))
    down[:half], down[half:depth] = np.cos(angle) * scale, -np.sin(angle) * scale
    down[depth] = np.where(z % 2 == 0, 1, -1) * scale
    twice = np.where(kz == 0, 1, 2)[None, :]
    up = np.concatenate([np.cos(angle.T) * twice, -np.sin(angle.T) * twice], 1) * scale
    kx = np.arange(width)
    turn = 2 * np.pi * (kx[:, None] * kx[None, :] % width) / width
    across = np.concatenate([np.cos(turn), np.sin(turn)], 1) / math.sqrt(width)
    fz, fx = signed(depth), signed(width)
    theta = np.degrees(np.arctan2(fz[:, None] * np.where(fx >= 0, 1, -1)[None, :], np.abs(fx)[None, :] * 1.0))
    mirror = theta[(-z) % depth][:, (-kx) % width]
    rows = np.minimum(np.arange(half + 8), half)
    theta, mirror = theta[rows], mirror[rows]
    mirror[0], mirror[half:] = theta[0], theta[half:]
    shift = 2 * np.pi * (rows[:, None] * np.arange(LANES)[None, :] % depth) / depth
    wedge = [np.exp(theta / SOFTNESS), np.exp(-theta / SOFTNESS), np.exp(mirror / SOFTNESS), np.exp(-mirror / SOFTNESS)]
    count = np.zeros((depth + 8, LANES))
    count[:depth], count[depth : depth + 2] = 2, 1
    count[0] = count[half] = 1
    single = np.concatenate(wedge + [np.cos(shift), np.sin(shift), count, np.cos(turn), np.sin(turn)], 0)
    return split(down), split(across), split(up), single.astype(np.float32)


def split(table):
    table = table.astype(np.float32)
    high = table.astype(BF16)
    low = (table - high.astype(np.float32)).astype(BF16)
    return np.concatenate([high, low], 0)


def halves(value):
    high = value.astype(BF16)
    return high, (value - high.astype(F32)).astype(BF16)


def mul(a, b):
    return jnp.dot(a, b, preferred_element_type=F32)


def by_table(value, table):
    rows = table.shape[0] // 2
    high, low = halves(value)
    top = table[:rows]
    return mul(high, top) + mul(low, top) + mul(high, table[rows:])


def table_by(table, value):
    rows = table.shape[0] // 2
    high, low = halves(value)
    top = table[:rows]
    return mul(top, high) + mul(top, low) + mul(table[rows:], high)


def refine(
    slabs, ring, v_hbm, s_hbm, down_hbm, across_hbm, up_hbm, single_hbm, low_ref, high_ref, shift_ref, out_ref, mis_ref,
    v_ref, s_ref, down_ref, across_ref, up_ref, single, u_ref, blocks,
    power_out, power_in, block_in, tilt_out, tilt_in, tilts_out, tilts_in, rows_in, factors, part, parts_in, own_out, own_in,
    some_out, some_in, more_out, more_in, plane, pieces_in, planes_in, s_load, s_volume,
    s_power, r_power, s_block, r_block, s_tilt, r_tilt, s_tilts, r_tilts, s_rows, r_rows, s_part, r_part, s_own, r_own,
    s_some, r_some, s_more, r_more, s_piece, r_piece, s_plane, r_plane,
):
    depth = slabs * 8
    half = depth // 2
    tall = half + 8
    copies = ring // 2
    subs = float(GROUP * copies * 2)
    cells = float(depth * depth * LANES)
    batch, slab = lax.axis_index("batch"), lax.axis_index("slab")
    x, y = batch // ring, batch % ring
    r, p = y // 2, y % 2
    g = x * 2 + p

    def at_slab(t):
        return (batch, t)

    def at_group(k):
        return (lax.div(k, 2) * ring + r * 2 + lax.rem(k, 2), slab)

    def at_copy(k):
        return (x * ring + k * 2 + p, slab)

    def each(count, me, act, unroll=True):
        if unroll:
            for off in sorted(range(1, count), key=lambda off: abs(off - count / 2)):
                act(lax.rem(me + off, count))
            return

        def step(k, carry):
            act(lax.rem(me + 1 + lax.rem(k + count // 4, count - 1), count))
            return carry

        if count > 1:
            lax.fori_loop(0, count - 1, step, 0)

    def exchange(count, me, device, source, target, send, recv, unroll=True):
        def copy(k, slot):
            return pltpu.make_async_remote_copy(
                src_ref=source(k), dst_ref=target(slot), send_sem=send.at[k], recv_sem=recv.at[slot],
                device_id=device(k), device_id_type=MESH,
            )

        return (
            lambda: each(count, me, lambda k: copy(k, me).start(), unroll),
            lambda: each(count, me, lambda k: copy(k, k).wait_recv(), unroll),
            lambda: each(count, me, lambda k: copy(k, me).wait_send(), False),
        )

    barrier = pltpu.get_barrier_semaphore()
    for count, me, device in ((slabs, slab, at_slab), (GROUP, g, at_group), (copies, r, at_copy)):
        each(count, me, lambda k, device=device: pl.semaphore_signal(
            barrier, inc=1, device_id=device(k), device_id_type=MESH))
    def volume_copy(k, again):
        return pltpu.make_async_copy(
            v_hbm.at[k], v_ref.at[pl.ds(pl.multiple_of(2 * depth * k + depth * again, depth), depth)], s_volume.at[again, k])

    loads = [
        pltpu.make_async_copy(source, target, s_load.at[k])
        for k, (source, target) in enumerate((
            (s_hbm, s_ref), (single_hbm, single), (down_hbm, down_ref), (across_hbm, across_ref), (up_hbm, up_ref)))
    ]

    def over(count, act):
        def step(k, carry):
            act(k)
            return carry

        lax.fori_loop(0, count, step, 0)

    for again in range(2):
        over(16, lambda k, again=again: volume_copy(k, again).start())
    for load in loads:
        load.start()
    for again in range(2):
        over(16, lambda k, again=again: volume_copy(k, again).wait())
    power = jnp.zeros((8, LANES), F32)
    for item in range(2):
        first = item * 16 * depth + depth - shift_ref[item, 1]

        def fill(t, power, item=item, first=first):
            for k in range(8):
                rows = v_ref[pl.ds(first + t * 8 + k, 8, stride=2 * depth), :]
                u_ref[t, k, item] = rows
                power = power + rows * rows
            return power

        power = lax.fori_loop(0, slabs, fill, power)
    power_out[0:1] = jnp.sum(power, axis=0, keepdims=True)
    pl.semaphore_wait(barrier, slabs - 1 + GROUP - 1 + copies - 1)

    powers = exchange(
        slabs, slab, at_slab, lambda k: power_out.at[0:1], lambda k: power_in.at[k, 0:1], s_power, r_power)
    block = exchange(slabs, slab, at_slab, lambda k: blocks.at[k], lambda k: block_in.at[k], s_block, r_block)
    tilt = exchange(GROUP, g, at_group, lambda k: tilt_out.at[0:2], lambda k: tilt_in.at[k, 0:2], s_tilt, r_tilt)
    tilts = exchange(copies, r, at_copy, lambda k: tilts_out, lambda k: tilts_in.at[k], s_tilts, r_tilts)
    own = exchange(copies, r, at_copy, lambda k: own_out, lambda k: own_in.at[k], s_own, r_own)
    piece = exchange(
        slabs, slab, at_slab, lambda k: plane.at[pl.ds(pl.multiple_of(k * 8, 8), 8)], lambda k: pieces_in.at[k], s_piece, r_piece)
    whole = exchange(GROUP, g, at_group, lambda k: pieces_in, lambda k: planes_in.at[k], s_plane, r_plane)

    def rows(c):
        first, number = lax.rem(x + 1 + c, XS) * 2, 2
        if c >= XS - 1:
            first, number = x * 2 + (1 - p if c == XS - 1 else p), 1
        return first, number, exchange(
            slabs, slab, at_slab, lambda k: u_ref.at[k, pl.ds(first, number)],
            lambda k: rows_in.at[pl.ds(first, number), :, k], s_rows.at[c], r_rows.at[c], False)

    def part_copy(k):
        return pltpu.make_async_remote_copy(
            src_ref=part.at[k], dst_ref=parts_in.at[g], send_sem=s_part.at[k], recv_sem=r_part.at[g],
            device_id=at_group(k), device_id_type=MESH)

    def part_wait(k):
        return pltpu.make_async_remote_copy(
            src_ref=part.at[k], dst_ref=parts_in.at[k], send_sem=s_part.at[k], recv_sem=r_part.at[k],
            device_id=at_group(k), device_id_type=MESH)

    def whole_wait(k):
        pltpu.make_async_remote_copy(
            src_ref=pieces_in, dst_ref=planes_in.at[k], send_sem=s_plane.at[k], recv_sem=r_plane.at[k],
            device_id=at_group(k), device_id_type=MESH).wait_recv()

    def sums_over(turn):
        return exchange(
            GROUP, g, at_group, lambda k: some_out.at[turn, 0:1], lambda k: some_in.at[turn, k, 0:1], s_some.at[turn], r_some.at[turn],
        ), exchange(
            slabs, slab, at_slab, lambda k: more_out.at[turn, 0:1], lambda k: more_in.at[turn, k, 0:1], s_more.at[turn], r_more.at[turn])

    powers[0]()
    for c in range(CHUNKS):
        rows(c)[2][0]()
    loads[0].wait()

    def cut(t, carry):
        blocks[t] = s_ref[pl.ds(t * 8 + g, 8, stride=depth), :]
        return carry

    lax.fori_loop(0, slabs, cut, 0)
    block[0]()
    block_in[slab] = blocks[slab]
    power_in[slab, 0:1] = power_out[0:1]
    for k in range(8):
        for item in range(2):
            rows_in[k, item, slab] = u_ref[slab, k, item]

    lane = lax.broadcasted_iota(jnp.int32, (half, LANES), 1)
    row = lax.broadcasted_iota(jnp.int32, (half, LANES), 0)
    here = lane % HALF == row
    left = lane < HALF
    tile_row = lax.broadcasted_iota(jnp.int32, (8, LANES), 0)
    wide = lax.broadcasted_iota(jnp.int32, (tall, LANES), 1)

    spot = lax.broadcasted_iota(jnp.int32, (8, LANES), 1)
    edge = jnp.where(spot == 0, low_ref[0].astype(F32), jnp.where(spot == 1, low_ref[1].astype(F32), 0.0))
    edge = jnp.where(spot == 2, -high_ref[0].astype(F32), jnp.where(spot == 3, -high_ref[1].astype(F32), edge))
    edge = jnp.exp(edge * (1 / SOFTNESS))
    loads[1].wait()

    def table(k):
        return single[k * tall : (k + 1) * tall]

    def weight(p_table, q_table, low, high):
        return 1.0 / ((1.0 + p_table * high) * (1.0 + q_table * low))

    for item in range(2):
        low, high = edge[0:1, item : item + 1], edge[0:1, item + 2 : item + 3]
        w = weight(table(0), table(1), low, high)
        dw = weight(table(2), table(3), low, high) - w
        pick = wide == shift_ref[item, 0]
        zc = jnp.sum(jnp.where(pick, table(4), 0.0), axis=1, keepdims=True)
        zs = jnp.sum(jnp.where(pick, table(5), 0.0), axis=1, keepdims=True)
        first = 6 * tall + depth + 8
        xc = single[pl.ds(first + shift_ref[item, 2], 1), :]
        xs = single[pl.ds(first + LANES + shift_ref[item, 2], 1), :]
        cosine, sine = zc * xc - zs * xs, zs * xc + zc * xs
        factors[item, 0], factors[item, 1] = w * cosine, w * sine
        factors[item, 2], factors[item, 3] = dw * cosine, dw * sine

    powers[1]()
    energy = power_in[0, 0:1]
    for k in range(1, slabs):
        energy = energy + power_in[k, 0:1]
    tilt_out[0:1] = edge[0:1]
    tilt_out[1:2] = energy
    tilt[0]()
    tilt_in[g, 0:2] = tilt_out[0:2]
    for load in loads[2:]:
        load.wait()
    down, across, up = down_ref[...], across_ref[...], up_ref[...]

    def chunk(c):
        first, number, moved = rows(c)
        moved[1]()
        stack = []
        for k in range(number):
            for item in range(2):
                stack.append(table_by(down, rows_in[first + k, item].reshape(depth, LANES)))
        product = by_table(jnp.concatenate(stack, 0), across)
        for k in range(number):
            re = im = re_last = im_last = d_re = d_im = 0.0
            for item in range(2):
                at = (k * 2 + item) * (depth + 8)
                c_top, c_low, c_last = (product[at + a : at + b, :LANES] for a, b in ((0, half), (half, depth), (depth, depth + 8)))
                s_top, s_low, s_last = (product[at + a : at + b, LANES:] for a, b in ((0, half), (half, depth), (depth, depth + 8)))
                a, b = c_top + s_low, c_low - s_top
                wc, ws = factors[item, 0, :half], factors[item, 1, :half]
                re, im = re + wc * a + ws * b, im + wc * b - ws * a
                wc, ws = factors[item, 2, :half], factors[item, 3, :half]
                d_re, d_im = d_re + wc * a + ws * b, d_im + wc * b - ws * a
                wc, ws = factors[item, 0, half:], factors[item, 1, half:]
                re_last, im_last = re_last + wc * c_last - ws * s_last, im_last - wc * s_last - ws * c_last

            def lying(d):
                column = jnp.where(left, d[:, 0:1], d[:, HALF : HALF + 1])
                return jnp.sum(jnp.where(here, column, 0.0), axis=0, keepdims=True)

            last = jnp.where(tile_row == 0, re_last[0:1], jnp.where(tile_row == 1, im_last[0:1], 0.0))
            last = jnp.where(tile_row == 2, lying(d_re), jnp.where(tile_row == 3, lying(d_im), last))
            part[first + k, 0:half], part[first + k, half:depth] = re, im
            part[first + k, depth:] = last
        return first

    def add_up(ref, count):
        total = ref[0]
        for k in range(1, count):
            total = total + ref[k]
        return total

    for c in range(CHUNKS):
        first = chunk(c)
        if c < XS - 1:
            part_copy(first + 1 - p).start()
            part_copy(first + p).start()
        elif c == XS - 1:
            part_copy(first).start()
        if c == 0:
            tilt[1]()
            tilts_out[0:8] = jnp.concatenate([tilt_in[k, 0:1] for k in range(GROUP)], 0)
            energy = tilt_in[0, 1:2]
            for k in range(1, GROUP):
                energy = energy + tilt_in[k, 1:2]
            tilts_out[8:16] = jnp.broadcast_to(energy, (8, LANES))
            tilts[0]()
            tilts_in[r] = tilts_out[...]
        if c == 2:
            tilts[1]()
            energy = tilts_in[0, 8:9]
            for k in range(1, copies):
                energy = energy + tilts_in[k, 8:9]

            def square(k, totals):
                total, mirrored = totals
                for j in range(GROUP):
                    for item in range(2):
                        low, high = tilts_in[k, j : j + 1, item : item + 1], tilts_in[k, j : j + 1, item + 2 : item + 3]
                        w = weight(table(0), table(1), low, high)
                        total = total + w * w
                        w = weight(table(2), table(3), low, high)
                        mirrored = mirrored + w * w
                return total, mirrored

            none = jnp.zeros((tall, LANES), F32)
            total, mirrored = lax.fori_loop(0, copies, square, (none, none))

    parts_in[g] = part[g]
    each(GROUP, g, lambda k: part_wait(k).wait_recv())
    own_out[...] = add_up(parts_in, GROUP)
    own[0]()
    own_in[r] = own_out[...]

    def stacked(d):
        return jnp.concatenate([d[:half], d[:half], jnp.where(tile_row < 2, d[half : half + 1], 0.0)], 0)

    d_one, d_two = stacked(total), stacked(mirrored)
    block[1]()
    support = block_in[...].reshape(depth, LANES)
    sign = jnp.where(lax.broadcasted_iota(jnp.int32, (depth, LANES), 0) % 2 == 0, 1.0, -1.0) * (1 / math.sqrt(depth))
    count = single[6 * tall : 6 * tall + depth + 8]
    powers[2](), block[2](), tilt[2](), tilts[2]()
    for c in range(CHUNKS):
        rows(c)[2][2]()
    own[1]()
    sums = add_up(own_in, copies)

    def standing(values):
        spread = jnp.where(here, values, 0.0)
        one = jnp.sum(jnp.where(left, spread, 0.0), axis=1, keepdims=True)
        two = jnp.sum(jnp.where(left, 0.0, spread), axis=1, keepdims=True)
        return jnp.where(lane == 0, one, jnp.where(lane == HALF, two, 0.0))

    change = jnp.concatenate(
        [standing(sums[depth + 2 : depth + 3]), standing(sums[depth + 3 : depth + 4]), jnp.zeros((8, LANES), F32)], 0)
    sums = jnp.concatenate([sums[:depth], jnp.where(tile_row < 2, sums[depth:], 0.0)], 0)
    mean = jnp.zeros((depth + 8, LANES), F32)
    power = jnp.sum(energy, axis=(0, 1), keepdims=True)
    misfit = power * (1.0 / (subs * cells))
    mis_ref[0] = jnp.sum(misfit)
    for turn in range(ITERS):
        damping = REG_WEIGHT * subs * misfit + FLOOR_VALUE
        one, two = 0.5 / (d_one + damping), 0.5 / (d_two + damping)
        update = mean - mean * (d_one * one + d_two * two) + (one + two) * sums + two * change
        product = by_table(update, across)
        re = product[:half, :LANES] - product[half:depth, LANES:]
        im = product[half:depth, :LANES] + product[:half, LANES:]
        last = product[depth : depth + 1, :LANES] - product[depth + 1 : depth + 2, LANES:]
        field = table_by(up, jnp.concatenate([re, im], 0)) + sign * last
        if turn + 1 == ITERS:
            break
        product = by_table(table_by(down, support * field), across)
        last = jnp.where(tile_row == 0, product[depth : depth + 1, :LANES], -product[depth : depth + 1, LANES:])
        mean = jnp.concatenate([
            product[:half, :LANES] + product[half:depth, LANES:],
            product[half:depth, :LANES] - product[:half, LANES:],
            jnp.where(tile_row < 2, last, 0.0)], 0)
        terms = count * mean * (0.5 * (d_one + d_two) * mean - 2.0 * sums - change)
        some_out[turn, 0:1] = jnp.sum(terms, axis=0, keepdims=True)
        some, more = sums_over(turn)
        some[0]()
        some_in[turn, g, 0:1] = some_out[turn, 0:1]
        if turn == 0:
            own[2]()
            each(GROUP, g, lambda k: part_wait(k).wait_send(), False)
        some[1]()
        more_out[turn, 0:1] = add_up(some_in.at[turn, :, 0:1], GROUP)
        more[0]()
        more_in[turn, slab, 0:1] = more_out[turn, 0:1]
        more[1]()
        misfit = (power + jnp.sum(add_up(more_in.at[turn, :, 0:1], slabs), axis=(0, 1), keepdims=True)) * (1.0 / (subs * cells))
        mis_ref[turn + 1] = jnp.sum(misfit)
    plane[...] = field
    piece[0]()
    pieces_in[slab] = plane[pl.ds(pl.multiple_of(slab * 8, 8), 8)]

    piece[1]()
    whole[0]()

    def place(k, source):
        for j in range(slabs):
            out_ref[pl.ds(j * 8 + k, 8, stride=depth), :] = source[j]

    place(g, pieces_in)
    for turn in range(ITERS - 1):
        sums_over(turn)[0][2](), sums_over(turn)[1][2]()
    piece[2]()

    def arrived(k):
        whole_wait(k)
        place(k, planes_in.at[k])

    each(GROUP, g, arrived)
    whole[2]()


def body(volumes, tilt_low, tilt_high, shifts, support):
    slabs, ring = lax.axis_size("slab"), lax.axis_size("batch") // XS
    layer, ys, width = support.shape
    depth, copies, tall = layer * slabs, ring // 2, slabs * 8 + 8
    vmem, smem, hbm = (pl.BlockSpec(memory_space=space) for space in (pltpu.VMEM, pltpu.SMEM, pl.ANY))
    down, across, up, single = (jnp.asarray(table) for table in tables(depth, width))
    dma = pltpu.SemaphoreType.DMA

    def buffer(*shape):
        return pltpu.VMEM((*shape, LANES), F32)

    field, misfits = pl.pallas_call(
        functools.partial(refine, slabs, ring),
        out_shape=(jax.ShapeDtypeStruct((layer * ys, width), F32), jax.ShapeDtypeStruct((ITERS,), F32)),
        in_specs=[hbm] * 6 + [smem] * 3,
        out_specs=(vmem, smem),
        scratch_shapes=[
            buffer(2 * layer * 2 * ys), buffer(layer * ys), pltpu.VMEM(down.shape, BF16), pltpu.VMEM(across.shape, BF16),
            pltpu.VMEM(up.shape, BF16), buffer(single.shape[0]), buffer(slabs, 8, 2, 8), buffer(slabs, 8),
            buffer(8), buffer(slabs, 8), buffer(slabs, 8), buffer(8), buffer(GROUP, 8), buffer(16), buffer(copies, 16),
            buffer(8, 2, slabs, 8), buffer(2, 4, depth // 2 + 8),
            buffer(GROUP, tall), buffer(GROUP, tall), buffer(tall), buffer(copies, tall),
            buffer(2, 8), buffer(2, GROUP, 8), buffer(2, 8), buffer(2, slabs, 8),
            buffer(depth), buffer(slabs, 8), buffer(GROUP, slabs, 8), dma((5,)), dma((2, 16)),
            dma((slabs,)), dma((slabs,)), dma((slabs,)), dma((slabs,)), dma((GROUP,)), dma((GROUP,)), dma((copies,)), dma((copies,)),
            dma((CHUNKS, slabs)), dma((CHUNKS, slabs)), dma((GROUP,)), dma((GROUP,)), dma((copies,)), dma((copies,)),
            dma((2, GROUP)), dma((2, GROUP)), dma((2, slabs)), dma((2, slabs)),
            dma((slabs,)), dma((slabs,)), dma((GROUP,)), dma((GROUP,)),
        ],
        compiler_params=pltpu.CompilerParams(collective_id=0, has_side_effects=True),
        name="refine",
    )(volumes.reshape(2 * layer, ys, width), support.reshape(layer * ys, width), down, across, up, single, tilt_low, tilt_high, shifts)
    return support * field.reshape(layer, ys, width), misfits


def solution(mesh):
    placed = (
        P("batch", "slab", None, None),
        P("batch"),
        P("batch"),
        P("batch", None),
        P("slab", None, None),
    )
    return jax.shard_map(
        body, mesh=mesh, in_specs=placed, out_specs=(P("slab", None, None), P()), check_vma=False
    )
```

time: 104 us -> 92 us (0.88)
  Pallas kernels: 98.5 us -> 88.8 us
  local copies, waits for them, and re-layouts: 4.42 us -> 0.52 us
  other arithmetic: 0.08 us -> 1.89 us
    pallas_call x1, Pallas kernels: 94.5 us -> 88.8 us  [body(): pl.pallas_call(functools.partial(refine, slabs, ring), out_shape=(jax.Sha...]
    pallas_call x1 -> x0, Pallas kernels: 3.95 us -> none  [body(): pl.pallas_call(functools.partial(arrange, slabs), out_shape=(jax.ShapeDty...]
    unnamed x7 -> x5, local copies, waits for them, and re-layouts: 3.2 us -> 0.52 us
    mul x0 -> x1, other arithmetic: none -> 1.89 us  [body(): return (support * field.reshape(layer, ys, width), misfits)]
where the time goes in v1:
time: 92 us; the launch traced here: 91.8 us
  Pallas kernels  88.8 us (97%)
  other arithmetic  1.89 us (2%)
    pallas_call x1, Pallas kernels, body(): pl.pallas_call(functools.partial(refine, slabs, ring), out_shape=(jax.Sha...  88.8 us
    mul x1, other arithmetic, body(): return (support * field.reshape(layer, ys, width), misfits)  1.89 us

profile of v1, /device:TPU:1, one launch (start us, length us, event | category | flops | bytes accessed | tf_op | source)
XLA Modules:
  0.0 91.8 jit_solution(7657886370031346774)
XLA Ops:
  0.6 0.0 copy-start
  0.6 88.8 %refine.1 = (f32[1024,128]{1,0:T(8,128)}, f32[3]{0:T(128)}) custom-call(f32[16,128,128]{2,1,0:T(8,128)} %bitcast.4, f32[1024,128]{1,0:T(8,128)} %bitcast.3, bf16[272,128]{1,0:T(8,128)(2,1)} %constant.8.clone.down_hbm, bf16[256,256]{1,0:T(8,128)(2,1)} %constant.9.clone.across_hbm, bf16[256,128]{1,0:T(8,128)(2,1)} %constant.10.clone.up_hbm, ...), custom_call_target="tpu_custom_call" | custom-call | tf_op jit(solution)/shard_map/refine/pallas_call | solution.py:460
  89.4 0.0 copy-done
  89.4 0.0 copy-start.1
  89.4 1.9 %mul.3 = f32[8,128,128]{2,1,0:T(8,128)} multiply(f32[8,128,128]{2,1,0:T(8,128)S(1)} %copy-done, f32[8,128,128]{2,1,0:T(8,128)} %bitcast.5) | non-fusion elementwise | flops 131072 | bytes 1572864 | tf_op jit(solution)/shard_map/mul | solution.py:481
  91.3 0.0 copy-done.1
  91.3 0.5 copy.12
Async XLA Ops:
  0.6 88.8 %copy-start = (f32[8,128,128]{2,1,0:T(8,128)S(1)}, f32[8,128,128]{2,1,0:T(8,128)}, u32[]{:S(2)}) copy-start(f32[8,128,128]{2,1,0:T(8,128)} %param.13) | copy-start | bytes 1572868
  89.4 1.9 %copy-start.1 = (f32[3]{0:T(128)S(1)}, f32[3]{0:T(128)}, u32[]{:S(2)}) copy-start(f32[3]{0:T(128)} %get-tuple-element.9) | copy-start | bytes 40

commit v2 on v1

--- a/solution.py
+++ b/solution.py
@@ -19,6 +19,7 @@
 XS = 4
 GROUP = XS * 2
 CHUNKS = 5
+BATCHES = [(0, 3), (3, 5), (5, 8)]
 F32 = jnp.float32
 BF16 = jnp.bfloat16
 
@@ -53,41 +54,33 @@
     count[:depth], count[depth : depth + 2] = 2, 1
     count[0] = count[half] = 1
     single = np.concatenate(wedge + [np.cos(shift), np.sin(shift), count, np.cos(turn), np.sin(turn)], 0)
-    return split(down), split(across), split(up), single.astype(np.float32)
-
-
-def split(table):
+    return split(down, 1), split(across, 0), split(up, 1), single.astype(np.float32)
+
+
+def split(table, axis):
     table = table.astype(np.float32)
     high = table.astype(BF16)
     low = (table - high.astype(np.float32)).astype(BF16)
-    return np.concatenate([high, low], 0)
-
-
-def halves(value):
+    return np.concatenate([high, high, low], axis)
+
+
+def thirds(value, axis):
     high = value.astype(BF16)
-    return high, (value - high.astype(F32)).astype(BF16)
-
-
-def mul(a, b):
-    return jnp.dot(a, b, preferred_element_type=F32)
+    low = (value - high.astype(F32)).astype(BF16)
+    return jnp.concatenate([high, low, high], axis)
 
 
 def by_table(value, table):
-    rows = table.shape[0] // 2
-    high, low = halves(value)
-    top = table[:rows]
-    return mul(high, top) + mul(low, top) + mul(high, table[rows:])
+    return jnp.dot(thirds(value, 1), table, preferred_element_type=F32)
 
 
 def table_by(table, value):
-    rows = table.shape[0] // 2
-    high, low = halves(value)
-    top = table[:rows]
-    return mul(top, high) + mul(top, low) + mul(table[rows:], high)
+    return jnp.dot(table, thirds(value, 0), preferred_element_type=F32)
 
 
 def refine(
-    slabs, ring, v_hbm, s_hbm, down_hbm, across_hbm, up_hbm, single_hbm, low_ref, high_ref, shift_ref, out_ref, mis_ref,
+    slabs, ring, v_hbm, s_hbm, down_hbm, across_hbm, up_hbm, single_hbm, low_hbm, high_hbm, shift_hbm, out_ref, mis_ref,
+    low_ref, high_ref, shift_ref,
     v_ref, s_ref, down_ref, across_ref, up_ref, single, u_ref, blocks,
     power_out, power_in, block_in, tilt_out, tilt_in, tilts_out, tilts_in, rows_in, factors, part, parts_in, own_out, own_in,
     some_out, some_in, more_out, more_in, plane, pieces_in, planes_in, s_load, s_volume,
@@ -151,7 +144,8 @@
     loads = [
         pltpu.make_async_copy(source, target, s_load.at[k])
         for k, (source, target) in enumerate((
-            (s_hbm, s_ref), (single_hbm, single), (down_hbm, down_ref), (across_hbm, across_ref), (up_hbm, up_ref)))
+            (s_hbm, s_ref), (single_hbm, single), (down_hbm, down_ref), (across_hbm, across_ref), (up_hbm, up_ref),
+            (low_hbm, low_ref), (high_hbm, high_ref), (shift_hbm, shift_ref)))
     ]
 
     def over(count, act):
@@ -161,10 +155,14 @@
 
         lax.fori_loop(0, count, step, 0)
 
+    for load in loads[5:]:
+        load.start()
     for again in range(2):
         over(16, lambda k, again=again: volume_copy(k, again).start())
-    for load in loads:
+    for load in loads[:5]:
         load.start()
+    for load in loads[5:]:
+        load.wait()
     for again in range(2):
         over(16, lambda k, again=again: volume_copy(k, again).wait())
     power = jnp.zeros((8, LANES), F32)
@@ -188,9 +186,34 @@
     tilt = exchange(GROUP, g, at_group, lambda k: tilt_out.at[0:2], lambda k: tilt_in.at[k, 0:2], s_tilt, r_tilt)
     tilts = exchange(copies, r, at_copy, lambda k: tilts_out, lambda k: tilts_in.at[k], s_tilts, r_tilts)
     own = exchange(copies, r, at_copy, lambda k: own_out, lambda k: own_in.at[k], s_own, r_own)
-    piece = exchange(
-        slabs, slab, at_slab, lambda k: plane.at[pl.ds(pl.multiple_of(k * 8, 8), 8)], lambda k: pieces_in.at[k], s_piece, r_piece)
-    whole = exchange(GROUP, g, at_group, lambda k: pieces_in, lambda k: planes_in.at[k], s_plane, r_plane)
+    chips, chip, core = slabs // 2, lax.div(slab, 2), lax.rem(slab, 2)
+    around = sorted(range(chips), key=lambda d: min(d, chips - d))
+
+    def piece(place, there):
+        target = lax.rem(chip + around[place], chips) * 2 + there
+        slot = around.index((chips - around[place]) % chips) * 2 + core
+        return pltpu.make_async_remote_copy(
+            src_ref=plane.at[pl.ds(pl.multiple_of(target * 8, 8), 8)], dst_ref=pieces_in.at[slot],
+            send_sem=s_piece.at[place * 2 + there], recv_sem=r_piece.at[slot], device_id=at_slab(target), device_id_type=MESH)
+
+    def pieces(act, places):
+        for place in places:
+            for there in ((1 - core,) if place == 0 else (0, 1)):
+                act(place, there)
+
+    def piece_wait(place, there):
+        pltpu.make_async_remote_copy(
+            src_ref=plane.at[0:8], dst_ref=pieces_in.at[place * 2 + there], send_sem=s_piece.at[place * 2 + there],
+            recv_sem=r_piece.at[place * 2 + there], device_id=at_slab(slab), device_id_type=MESH).wait_recv()
+
+    def whole_copy(batch_of, k, slot):
+        cut = slice(batch_of[0] * 2, batch_of[1] * 2)
+        at = batches.index(batch_of)
+        return pltpu.make_async_remote_copy(
+            src_ref=pieces_in.at[cut], dst_ref=planes_in.at[slot, cut], send_sem=s_plane.at[at, k], recv_sem=r_plane.at[at, slot],
+            device_id=at_group(k), device_id_type=MESH)
+
+    batches = [cut for cut in BATCHES if cut[1] <= chips] or [(0, chips)]
 
     def rows(c):
         first, number = lax.rem(x + 1 + c, XS) * 2, 2
@@ -198,7 +221,7 @@
             first, number = x * 2 + (1 - p if c == XS - 1 else p), 1
         return first, number, exchange(
             slabs, slab, at_slab, lambda k: u_ref.at[k, pl.ds(first, number)],
-            lambda k: rows_in.at[pl.ds(first, number), :, k], s_rows.at[c], r_rows.at[c], False)
+            lambda k: rows_in.at[pl.ds(first, number), :, k], s_rows.at[c], r_rows.at[c])
 
     def part_copy(k):
         return pltpu.make_async_remote_copy(
@@ -209,11 +232,6 @@
         return pltpu.make_async_remote_copy(
             src_ref=part.at[k], dst_ref=parts_in.at[k], send_sem=s_part.at[k], recv_sem=r_part.at[k],
             device_id=at_group(k), device_id_type=MESH)
-
-    def whole_wait(k):
-        pltpu.make_async_remote_copy(
-            src_ref=pieces_in, dst_ref=planes_in.at[k], send_sem=s_plane.at[k], recv_sem=r_plane.at[k],
-            device_id=at_group(k), device_id_type=MESH).wait_recv()
 
     def sums_over(turn):
         return exchange(
@@ -279,7 +297,7 @@
     tilt_out[1:2] = energy
     tilt[0]()
     tilt_in[g, 0:2] = tilt_out[0:2]
-    for load in loads[2:]:
+    for load in loads[2:5]:
         load.wait()
     down, across, up = down_ref[...], across_ref[...], up_ref[...]
 
@@ -423,27 +441,31 @@
         misfit = (power + jnp.sum(add_up(more_in.at[turn, :, 0:1], slabs), axis=(0, 1), keepdims=True)) * (1.0 / (subs * cells))
         mis_ref[turn + 1] = jnp.sum(misfit)
     plane[...] = field
-    piece[0]()
-    pieces_in[slab] = plane[pl.ds(pl.multiple_of(slab * 8, 8), 8)]
-
-    piece[1]()
-    whole[0]()
-
-    def place(k, source):
-        for j in range(slabs):
-            out_ref[pl.ds(j * 8 + k, 8, stride=depth), :] = source[j]
-
-    place(g, pieces_in)
+    pieces(lambda place, there: piece(place, there).start(), range(chips))
+    pieces_in[core] = plane[pl.ds(pl.multiple_of(slab * 8, 8), 8)]
+
+    def place(k, source, cut):
+        for at in range(*cut):
+            for there in range(2):
+                j = lax.rem(chip + around[at], chips) * 2 + there
+                out_ref[pl.ds(j * 8 + k, 8, stride=depth), :] = source[at * 2 + there]
+
+    for cut in batches:
+        pieces(piece_wait, range(*cut))
+        each(GROUP, g, lambda k: whole_copy(cut, k, g).start())
     for turn in range(ITERS - 1):
         sums_over(turn)[0][2](), sums_over(turn)[1][2]()
-    piece[2]()
-
-    def arrived(k):
-        whole_wait(k)
-        place(k, planes_in.at[k])
-
-    each(GROUP, g, arrived)
-    whole[2]()
+    pieces(lambda place, there: piece(place, there).wait_send(), range(chips))
+    for cut in batches:
+        place(g, pieces_in, cut)
+
+        def arrived(k):
+            whole_copy(cut, k, k).wait_recv()
+            place(k, planes_in.at[k], cut)
+
+        each(GROUP, g, arrived)
+    for cut in batches:
+        each(GROUP, g, lambda k: whole_copy(cut, k, g).wait_send())
 
 
 def body(volumes, tilt_low, tilt_high, shifts, support):
@@ -459,21 +481,22 @@
 
     field, misfits = pl.pallas_call(
         functools.partial(refine, slabs, ring),
-        out_shape=(jax.ShapeDtypeStruct((layer * ys, width), F32), jax.ShapeDtypeStruct((ITERS,), F32)),
-        in_specs=[hbm] * 6 + [smem] * 3,
+        out_shape=(pltpu.VMEM((layer * ys, width), F32), jax.ShapeDtypeStruct((ITERS,), F32)),
+        in_specs=[hbm] * 9,
         out_specs=(vmem, smem),
         scratch_shapes=[
+            pltpu.SMEM((2,), jnp.int32), pltpu.SMEM((2,), jnp.int32), pltpu.SMEM((2, 3), jnp.int32),
             buffer(2 * layer * 2 * ys), buffer(layer * ys), pltpu.VMEM(down.shape, BF16), pltpu.VMEM(across.shape, BF16),
             pltpu.VMEM(up.shape, BF16), buffer(single.shape[0]), buffer(slabs, 8, 2, 8), buffer(slabs, 8),
             buffer(8), buffer(slabs, 8), buffer(slabs, 8), buffer(8), buffer(GROUP, 8), buffer(16), buffer(copies, 16),
             buffer(8, 2, slabs, 8), buffer(2, 4, depth // 2 + 8),
             buffer(GROUP, tall), buffer(GROUP, tall), buffer(tall), buffer(copies, tall),
             buffer(2, 8), buffer(2, GROUP, 8), buffer(2, 8), buffer(2, slabs, 8),
-            buffer(depth), buffer(slabs, 8), buffer(GROUP, slabs, 8), dma((5,)), dma((2, 16)),
+            buffer(depth), buffer(slabs, 8), buffer(GROUP, slabs, 8), dma((8,)), dma((2, 16)),
             dma((slabs,)), dma((slabs,)), dma((slabs,)), dma((slabs,)), dma((GROUP,)), dma((GROUP,)), dma((copies,)), dma((copies,)),
             dma((CHUNKS, slabs)), dma((CHUNKS, slabs)), dma((GROUP,)), dma((GROUP,)), dma((copies,)), dma((copies,)),
             dma((2, GROUP)), dma((2, GROUP)), dma((2, slabs)), dma((2, slabs)),
-            dma((slabs,)), dma((slabs,)), dma((GROUP,)), dma((GROUP,)),
+            dma((slabs,)), dma((slabs,)), dma((3, GROUP)), dma((3, GROUP)),
         ],
         compiler_params=pltpu.CompilerParams(collective_id=0, has_side_effects=True),
         name="refine",

time: 92 us -> 87.6 us (0.952)
  Pallas kernels: 88.8 us -> 85.4 us
  other arithmetic: 1.89 us -> 0.85 us
    pallas_call x1, Pallas kernels: 88.8 us -> 85.4 us  [body(): pl.pallas_call(functools.partial(refine, slabs, ring), out_shape=(pltpu.V...]
    mul x1, other arithmetic: 1.89 us -> 0.85 us  [body(): return (support * field.reshape(layer, ys, width), misfits)]
where the time goes in v2:
time: 87.6 us; the launch traced here: 87.5 us
  Pallas kernels  85.4 us (97%)
    pallas_call x1, Pallas kernels, body(): pl.pallas_call(functools.partial(refine, slabs, ring), out_shape=(pltpu.V...  85.4 us

profile of v2, /device:TPU:1, one launch (start us, length us, event | category | flops | bytes accessed | tf_op | source)
XLA Modules:
  0.0 87.5 jit_solution(14512068106332540011)
XLA Ops:
  0.6 0.0 copy-start
  0.6 85.4 %refine.1 = (f32[1024,128]{1,0:T(8,128)S(1)}, f32[3]{0:T(128)}) custom-call(f32[16,128,128]{2,1,0:T(8,128)} %bitcast.5, f32[1024,128]{1,0:T(8,128)} %bitcast.4, bf16[136,384]{1,0:T(8,128)(2,1)} %constant.8.clone.down_hbm, bf16[384,256]{1,0:T(8,128)(2,1)} %constant.9.clone.across_hbm, bf16[128,384]{1,0:T(8,128)(2,1)} %constant.10.clone.up_hbm, ...), custom_call_target="tpu_custom_call" | custom-call | tf_op jit(solution)/shard_map/refine/pallas_call | solution.py:482
  86.1 0.0 copy-done
  86.1 0.0 copy-start.1
  86.1 0.9 mul.3
  87.0 0.0 copy-done.1
  87.0 0.5 copy.12
Async XLA Ops:
  0.6 85.5 %copy-start = (f32[8,128,128]{2,1,0:T(8,128)S(1)}, f32[8,128,128]{2,1,0:T(8,128)}, u32[]{:S(2)}) copy-start(f32[8,128,128]{2,1,0:T(8,128)} %param.13) | copy-start | bytes 1572868
  86.1 0.9 copy-start.1

commit v3 on v2

--- a/solution.py
+++ b/solution.py
@@ -19,7 +19,7 @@
 XS = 4
 GROUP = XS * 2
 CHUNKS = 5
-BATCHES = [(0, 3), (3, 5), (5, 8)]
+BATCHES = [(0, 2), (2, 5), (5, 8)]
 F32 = jnp.float32
 BF16 = jnp.bfloat16
 
@@ -407,7 +407,7 @@
     mean = jnp.zeros((depth + 8, LANES), F32)
     power = jnp.sum(energy, axis=(0, 1), keepdims=True)
     misfit = power * (1.0 / (subs * cells))
-    mis_ref[0] = jnp.sum(misfit)
+    misfits = [misfit]
     for turn in range(ITERS):
         damping = REG_WEIGHT * subs * misfit + FLOOR_VALUE
         one, two = 0.5 / (d_one + damping), 0.5 / (d_two + damping)
@@ -439,7 +439,7 @@
         more_in[turn, slab, 0:1] = more_out[turn, 0:1]
         more[1]()
         misfit = (power + jnp.sum(add_up(more_in.at[turn, :, 0:1], slabs), axis=(0, 1), keepdims=True)) * (1.0 / (subs * cells))
-        mis_ref[turn + 1] = jnp.sum(misfit)
+        misfits.append(misfit)
     plane[...] = field
     pieces(lambda place, there: piece(place, there).start(), range(chips))
     pieces_in[core] = plane[pl.ds(pl.multiple_of(slab * 8, 8), 8)]
@@ -453,6 +453,8 @@
     for cut in batches:
         pieces(piece_wait, range(*cut))
         each(GROUP, g, lambda k: whole_copy(cut, k, g).start())
+    for turn in range(ITERS):
+        mis_ref[turn] = jnp.sum(misfits[turn])
     for turn in range(ITERS - 1):
         sums_over(turn)[0][2](), sums_over(turn)[1][2]()
     pieces(lambda place, there: piece(place, there).wait_send(), range(chips))

time: 87.6 us -> 87.4 us (level)
  no operation moved by 1% of the time
where the time goes in v3:
time: 87.4 us; the launch traced here: 87.2 us
  Pallas kernels  85.2 us (97%)
    pallas_call x1, Pallas kernels, body(): pl.pallas_call(functools.partial(refine, slabs, ring), out_shape=(pltpu.V...  85.2 us

profile of v3, /device:TPU:1, one launch (start us, length us, event | category | flops | bytes accessed | tf_op | source)
XLA Modules:
  0.0 87.2 jit_solution(8992167989675331929)
XLA Ops:
  0.6 0.0 copy-start
  0.6 85.2 %refine.1 = (f32[1024,128]{1,0:T(8,128)S(1)}, f32[3]{0:T(128)}) custom-call(f32[16,128,128]{2,1,0:T(8,128)} %bitcast.5, f32[1024,128]{1,0:T(8,128)} %bitcast.4, bf16[136,384]{1,0:T(8,128)(2,1)} %constant.8.clone.down_hbm, bf16[384,256]{1,0:T(8,128)(2,1)} %constant.9.clone.across_hbm, bf16[128,384]{1,0:T(8,128)(2,1)} %constant.10.clone.up_hbm, ...), custom_call_target="tpu_custom_call" | custom-call | tf_op jit(solution)/shard_map/refine/pallas_call | solution.py:484
  85.8 0.0 copy-done
  85.8 0.0 copy-start.1
  85.8 0.9 mul.3
  86.7 0.0 copy-done.1
  86.7 0.5 copy.12
Async XLA Ops:
  0.6 85.2 %copy-start = (f32[8,128,128]{2,1,0:T(8,128)S(1)}, f32[8,128,128]{2,1,0:T(8,128)}, u32[]{:S(2)}) copy-start(f32[8,128,128]{2,1,0:T(8,128)} %param.13) | copy-start | bytes 1572868
  85.8 0.9 copy-start.1

commit v4 on v3

--- a/solution.py
+++ b/solution.py
@@ -165,20 +165,18 @@
         load.wait()
     for again in range(2):
         over(16, lambda k, again=again: volume_copy(k, again).wait())
-    power = jnp.zeros((8, LANES), F32)
-    for item in range(2):
-        first = item * 16 * depth + depth - shift_ref[item, 1]
-
-        def fill(t, power, item=item, first=first):
-            for k in range(8):
-                rows = v_ref[pl.ds(first + t * 8 + k, 8, stride=2 * depth), :]
-                u_ref[t, k, item] = rows
-                power = power + rows * rows
+    begins = [item * 16 * depth + depth - shift_ref[item, 1] for item in range(2)]
+
+    def fill(first, number, power):
+        def step(t, power):
+            for k in range(number):
+                for item in range(2):
+                    rows = v_ref[pl.ds(begins[item] + t * 8 + first + k, 8, stride=2 * depth), :]
+                    u_ref[t, first + k, item] = rows
+                    power = power + rows * rows
             return power
 
-        power = lax.fori_loop(0, slabs, fill, power)
-    power_out[0:1] = jnp.sum(power, axis=0, keepdims=True)
-    pl.semaphore_wait(barrier, slabs - 1 + GROUP - 1 + copies - 1)
+        return lax.fori_loop(0, slabs, step, power)
 
     powers = exchange(
         slabs, slab, at_slab, lambda k: power_out.at[0:1], lambda k: power_in.at[k, 0:1], s_power, r_power)
@@ -239,8 +237,17 @@
         ), exchange(
             slabs, slab, at_slab, lambda k: more_out.at[turn, 0:1], lambda k: more_in.at[turn, k, 0:1], s_more.at[turn], r_more.at[turn])
 
+    power = jnp.zeros((8, LANES), F32)
+    for c in range(CHUNKS):
+        first, number, moved = rows(c)
+        power = fill(first, number, power)
+        if c == 0:
+            pl.semaphore_wait(barrier, slabs - 1 + GROUP - 1 + copies - 1)
+        if c < 1:
+            moved[0]()
+    power_out[0:1] = jnp.sum(power, axis=0, keepdims=True)
     powers[0]()
-    for c in range(CHUNKS):
+    for c in range(1, CHUNKS):
         rows(c)[2][0]()
     loads[0].wait()
 

time: 87.4 us -> 87.1 us (level)
  no operation moved by 1% of the time
where the time goes in v4:
time: 87.1 us; the launch traced here: 86.9 us
  Pallas kernels  84.9 us (97%)
    pallas_call x1, Pallas kernels, body(): pl.pallas_call(functools.partial(refine, slabs, ring), out_shape=(pltpu.V...  84.9 us

profile of v4, /device:TPU:1, one launch (start us, length us, event | category | flops | bytes accessed | tf_op | source)
XLA Modules:
  0.0 86.9 jit_solution(3963392945036992997)
XLA Ops:
  0.6 0.0 copy-start
  0.6 84.9 %refine.1 = (f32[1024,128]{1,0:T(8,128)S(1)}, f32[3]{0:T(128)}) custom-call(f32[16,128,128]{2,1,0:T(8,128)} %bitcast.5, f32[1024,128]{1,0:T(8,128)} %bitcast.4, bf16[136,384]{1,0:T(8,128)(2,1)} %constant.8.clone.down_hbm, bf16[384,256]{1,0:T(8,128)(2,1)} %constant.9.clone.across_hbm, bf16[128,384]{1,0:T(8,128)(2,1)} %constant.10.clone.up_hbm, ...), custom_call_target="tpu_custom_call" | custom-call | tf_op jit(solution)/shard_map/refine/pallas_call | solution.py:491
  85.5 0.0 copy-done
  85.6 0.0 copy-start.1
  85.6 0.9 mul.3
  86.4 0.0 copy-done.1
  86.4 0.5 copy.12
Async XLA Ops:
  0.6 84.9 %copy-start = (f32[8,128,128]{2,1,0:T(8,128)S(1)}, f32[8,128,128]{2,1,0:T(8,128)}, u32[]{:S(2)}) copy-start(f32[8,128,128]{2,1,0:T(8,128)} %param.13) | copy-start | bytes 1572868
  85.6 0.9 copy-start.1
